TPU v7x, 32 devices: a whole 2x2x4 slice. The times are simulated.
32 devices in a mesh: level: 4 (over y, core), blk: 8 (over z, x).
Axes of the slice: x: 2, y: 2, z: 4, core: 2. Of those that a mesh axis runs over, the one named last changes fastest.
Arguments:
- right_sides: bfloat16 [4, 8, 1024, 384], P('level', 'blk'), may hold values from -6 to 6
- diag_inverse: bfloat16 [4, 8, 1, 1024, 1024], P('level', 'blk'), may hold values from -0.1875 to 0.1875
- compress_basis: bfloat16 [4, 8, 1024, 256], P('level', 'blk'), may hold values from -0.1875 to 0.1875
- expand_basis: bfloat16 [4, 8, 1024, 256], P('level', 'blk'), may hold values from -0.125 to 0.125
- target_ranks: int32 [4, 8], P('level', 'blk'), may hold values from 32 to 256
- coupling: int32 [4, 8, 4, 8], replicated, may hold values 0 or 1
- section_order: int32 [4], replicated, may hold values from 0 to 3, each once
Outputs:
- solved: bfloat16 [4, 8, 1024, 384], P('level', 'blk')
All inputs are finite; a program needn't handle non-finite values.
Results may differ from a plain program's by a relative error of at most 0.015.
Values may be sent and summed in bfloat16 or wider, within the bound.
No kernel may reach another device: no remote copies, remote signals or barrier semaphores. Data moves between devices by JAX's collectives and lax.ppermute only.
A program may use at most 128 MiB of HBM per device.

v0:
```python
import jax
import jax.numpy as jnp
from jax import lax
from jax.sharding import PartitionSpec as P


def per_device(
    right_sides, diag_inverse, compress_basis, expand_basis, target_ranks, coupling, section_order
):
    levels = lax.axis_size("level")
    blocks = lax.axis_size("blk")
    my_level = lax.axis_index("level")
    my_block = lax.axis_index("blk")
    sides_here = right_sides[0, 0]
    inverse_here = diag_inverse[0, 0]
    basis_here = compress_basis[0, 0]
    expand_here = expand_basis[0, 0]
    rank_cap = basis_here.shape[1]
    seg_rows = sides_here.shape[0]
    sub_blocks = inverse_here.shape[0]
    block_rows = inverse_here.shape[1]
    kept_rows = (jnp.arange(rank_cap, dtype=jnp.int32) < target_ranks[0, 0])[:, None]
    my_section = section_order[my_level]
    level_ids = jnp.arange(levels, dtype=jnp.int32)

    def solve(incoming, columns):
        update = jnp.dot(
            expand_here, incoming.astype(jnp.bfloat16), preferred_element_type=jnp.float32
        )
        work_rows = (columns.astype(jnp.float32) - update).astype(jnp.bfloat16)
        work_rows = work_rows.reshape(sub_blocks, block_rows, columns.shape[1])
        solved_rows = jnp.einsum(
            "jab,jbr->jar", inverse_here, work_rows, preferred_element_type=jnp.float32
        )
        solved_rows = solved_rows.astype(jnp.bfloat16).reshape(seg_rows, columns.shape[1])
        coef_rows = lax.dot_general(
            basis_here, solved_rows, (((0,), (0,)), ((), ())), preferred_element_type=jnp.float32
        )
        coef_rows = jnp.where(kept_rows, coef_rows, 0.0).astype(jnp.bfloat16)
        return (solved_rows, coef_rows)

    def advance(carry_state, level_step, columns):
        incoming, solved_rows, coef_rows = carry_state
        solved_rows, coef_rows = lax.cond(
            my_section == level_step,
            lambda: solve(incoming, columns),
            lambda: (solved_rows, coef_rows),
        )
        if level_step == levels - 1:
            return (incoming, solved_rows, coef_rows)
        root_level = jnp.sum(jnp.where(section_order == level_step, level_ids, 0))
        is_later = (my_section > level_step).astype(jnp.float32)
        width_now = columns.shape[1]
        masked = jnp.where(my_level == root_level, coef_rows.astype(jnp.float32), 0.0)
        share = lax.psum_scatter(
            masked.astype(jnp.bfloat16), "level", scatter_dimension=1, tiled=True
        )
        share_cols = share.shape[1]
        gathered = lax.all_gather(share[None], "blk", axis=0, tiled=True)
        dest_weights = coupling[:, my_block, root_level, :].astype(jnp.bfloat16)
        sums = jnp.dot(
            dest_weights, gathered.reshape(blocks, -1), preferred_element_type=jnp.float32
        )
        sums = sums.reshape(levels, rank_cap, share_cols)
        arrived = lax.all_to_all(sums, "level", split_axis=0, concat_axis=2, tiled=True)
        arrived = arrived.reshape(rank_cap, width_now)
        return (incoming + is_later * arrived, solved_rows, coef_rows)

    width_now = sides_here.shape[1]
    carry_state = (
        jnp.zeros((rank_cap, width_now), jnp.float32),
        jnp.zeros((seg_rows, width_now), jnp.bfloat16),
        jnp.zeros((rank_cap, width_now), jnp.bfloat16),
    )
    for level_step in range(levels):
        carry_state = advance(carry_state, level_step, sides_here)
    result = carry_state[1]
    return result[None, None]


def solution(mesh):
    return jax.shard_map(
        per_device,
        mesh=mesh,
        in_specs=(
            P("level", "blk", None, None),
            P("level", "blk", None, None, None),
            P("level", "blk", None, None),
            P("level", "blk", None, None),
            P("level", "blk"),
            P(),
            P(),
        ),
        out_specs=P("level", "blk", None, None),
        check_vma=False,
    )
```

profile of v0, /device:TPU:0, one launch (start us, length us, event | category | flops | bytes accessed | tf_op | source)
XLA Modules:
  0.0 239.5 jit_solution(6065074242285254970)
XLA Ops:
  6.5 1.5 fusion.52
  8.0 1.3 dynamic_slice.12
  10.0 1.4 copy.24
  12.8 1.0 conditional.4
  12.8 1.0 broadcast_in_dim.52
  13.8 0.7 select_convert_fusion.2
  20.5 0.8 dynamic-slice_convert_fusion
  21.4 18.6 %reduce-scatter.4.cloned.1.call-done = bf16[256,96]{0,1:T(8,128)(2,1)} async-done(((bf16[256,384]{0,1:T(8,128)(2,1)}), bf16[256,96]{0,1:T(8,128)(2,1)}) %reduce-scatter.4.cloned.1.call-update) | async-done | bytes 49168 | tf_op jit(solution)/shard_map/reduce_scatter | solution.py:55
  39.9 31.4 %all-gather = bf16[2048,96]{0,1:T(8,128)(2,1)S(1)} all-gather(bf16[256,96]{0,1:T(8,128)(2,1)} %reduce-scatter.4.cloned.1.call-done), channel_id=2, replica_groups=mesh['level'=4,'blk'=8] {'blk'}, dimensions={0}, use_global_device_ids=true | all-gather | bytes 442368 | tf_op jit(solution)/shard_map/all_gather | solution.py:59
  71.7 0.7 reshape.110
  73.5 0.8 copy.27
  74.4 3.5 %all-to-all-start = ((f32[4,256,96]{1,2,0:T(8,128)}), f32[4,256,96]{1,2,0:T(8,128)S(1)}, u32[]{:S(2)}, u32[]{:S(2)}) async-start(f32[4,256,96]{1,2,0:T(8,128)} %copy.27), calls=%async_computation.1 | async-start | bytes 786432 | tf_op jit(solution)/shard_map/all_to_all | solution.py:65
  79.9 5.3 %all-to-all-done = f32[4,256,96]{1,2,0:T(8,128)S(1)} async-done(((f32[4,256,96]{1,2,0:T(8,128)}), f32[4,256,96]{1,2,0:T(8,128)S(1)}, u32[]{:S(2)}, u32[]{:S(2)}) %all-to-all-start) | async-done | bytes 393248 | tf_op jit(solution)/shard_map/all_to_all | solution.py:65
  85.3 0.7 select_convert_fusion.1
  86.0 25.5 %reduce-scatter.6.cloned.1.call-done = bf16[256,96]{0,1:T(8,128)(2,1)} async-done(((bf16[256,384]{0,1:T(8,128)(2,1)}), bf16[256,96]{0,1:T(8,128)(2,1)}) %reduce-scatter.6.cloned.1.call-update) | async-done | bytes 49168 | tf_op jit(solution)/shard_map/reduce_scatter | solution.py:55
  111.5 31.5 %all-gather.1 = bf16[2048,96]{0,1:T(8,128)(2,1)S(1)} all-gather(bf16[256,96]{0,1:T(8,128)(2,1)} %reduce-scatter.6.cloned.1.call-done), channel_id=3, replica_groups=mesh['level'=4,'blk'=8] {'blk'}, dimensions={0}, use_global_device_ids=true | all-gather | bytes 442368 | tf_op jit(solution)/shard_map/all_gather | solution.py:59
  143.2 0.7 reshape.111
  144.0 0.5 dot_general.62
  145.1 0.8 copy.32
  145.9 3.6 %all-to-all-start.1 = ((f32[4,256,96]{1,2,0:T(8,128)}), f32[4,256,96]{1,2,0:T(8,128)S(1)}, u32[]{:S(2)}, u32[]{:S(2)}) async-start(f32[4,256,96]{1,2,0:T(8,128)} %copy.32), calls=%async_computation.3 | async-start | bytes 786432 | tf_op jit(solution)/shard_map/all_to_all | solution.py:65
  151.6 5.3 %all-to-all-done.1 = f32[4,256,96]{1,2,0:T(8,128)S(1)} async-done(((f32[4,256,96]{1,2,0:T(8,128)}), f32[4,256,96]{1,2,0:T(8,128)S(1)}, u32[]{:S(2)}, u32[]{:S(2)}) %all-to-all-start.1) | async-done | bytes 393248 | tf_op jit(solution)/shard_map/all_to_all | solution.py:65
  157.0 0.7 select_convert_fusion
  157.8 24.9 %reduce-scatter.8.cloned.1.call-done = bf16[256,96]{0,1:T(8,128)(2,1)} async-done(((bf16[256,384]{0,1:T(8,128)(2,1)}), bf16[256,96]{0,1:T(8,128)(2,1)}) %reduce-scatter.8.cloned.1.call-update) | async-done | bytes 49168 | tf_op jit(solution)/shard_map/reduce_scatter | solution.py:55
  182.7 31.6 %all-gather.2 = bf16[2048,96]{0,1:T(8,128)(2,1)S(1)} all-gather(bf16[256,96]{0,1:T(8,128)(2,1)} %reduce-scatter.8.cloned.1.call-done), channel_id=4, replica_groups=mesh['level'=4,'blk'=8] {'blk'}, dimensions={0}, use_global_device_ids=true | all-gather | bytes 442368 | tf_op jit(solution)/shard_map/all_gather | solution.py:59
  214.6 0.7 reshape.112
  215.3 0.5 dot_general.65
  216.5 0.8 copy.37
  217.3 3.5 %all-to-all-start.2 = ((f32[4,256,96]{1,2,0:T(8,128)}), f32[4,256,96]{1,2,0:T(8,128)S(1)}, u32[]{:S(2)}, u32[]{:S(2)}) async-start(f32[4,256,96]{1,2,0:T(8,128)} %copy.37), calls=%async_computation.5 | async-start | bytes 786432 | tf_op jit(solution)/shard_map/all_to_all | solution.py:65
  221.4 6.7 %all-to-all-done.2 = f32[4,256,96]{1,2,0:T(8,128)S(1)} async-done(((f32[4,256,96]{1,2,0:T(8,128)}), f32[4,256,96]{1,2,0:T(8,128)S(1)}, u32[]{:S(2)}, u32[]{:S(2)}) %all-to-all-start.2) | async-done | bytes 393248 | tf_op jit(solution)/shard_map/all_to_all | solution.py:65
  228.1 3.9 %conditional.7 = (bf16[1,1,1024,384]{3,2,1,0:T(8,128)(2,1)S(1)}) conditional(s32[]{:T(128)} %bitcast.17, bf16[1024,384]{0,1:T(8,128)(2,1)} %get-tuple-element.110, (bf16[1024,384]{0,1:T(8,128)(2,1)S(1)}, s32[1]{0:T(128)}, f32[1,256,4,96]{1,3,2,0:T(8,128)S(1)}, f32[256,384]{0,1:T(8,128)S(1)}, bf16[1024,256]{1,0:T(8,128)(2,1)S(1)}, ...), branch_computations={%region_12.13_spmd, %region_13.14_spmd} | conditional | flops 1008500736 | bytes 7733274 | solution.py:44
  228.9 2.8 %fusion.6 = bf16[1,1,1024,384]{2,3,1,0:T(8,128)(2,1)S(1)} fusion(bf16[1,1024,1024]{2,1,0:T(8,128)(2,1)} %get-tuple-element.103, bf16[1024,384]{0,1:T(8,128)(2,1)S(1)} %get-tuple-element.98, bf16[256,384]{0,1:T(8,128)(2,1)S(1)} %fusion.9, bf16[1024,256]{1,0:T(8,128)(2,1)S(1)} %get-tuple-element.102), kind=kOutput, calls=%fused_computation.5 | convolution fusion | flops 1008205824 | bytes 4390912 | tf_op jit(solution)/shard_map/cond/branch_1_fun/jab,jbr->jar/dot_general | solution.py:32
  232.1 0.9 copy-done
  (35 shorter events, 3.8 us)
Async XLA Ops:
  6.5 6.2 %copy-start.2 = (bf16[1,1,1024,256]{3,2,1,0:T(8,128)(2,1)S(1)}, bf16[1,1,1024,256]{3,2,1,0:T(8,128)(2,1)}, u32[]{:S(2)}) copy-start(bf16[1,1,1024,256]{3,2,1,0:T(8,128)(2,1)} %param.18) | copy-start | bytes 1572868
  6.5 6.2 %copy-start.1 = (bf16[1,1,1024,256]{3,2,1,0:T(8,128)(2,1)S(1)}, bf16[1,1,1024,256]{3,2,1,0:T(8,128)(2,1)}, u32[]{:S(2)}) copy-start(bf16[1,1,1024,256]{3,2,1,0:T(8,128)(2,1)} %param.17) | copy-start | bytes 1572868
  6.5 33.4 %reduce-scatter.4.cloned.1.call-start = ((), (), s32[]{:S(2)}) async-start(), calls=%async_computation.6 | async-start | bytes 245760 | tf_op jit(solution)/shard_map/reduce_scatter | solution.py:55
  74.4 10.8 %all-to-all-start = ((f32[4,256,96]{1,2,0:T(8,128)}), f32[4,256,96]{1,2,0:T(8,128)S(1)}, u32[]{:S(2)}, u32[]{:S(2)}) async-start(f32[4,256,96]{1,2,0:T(8,128)} %copy.27), calls=%async_computation.1 | async-start | bytes 786432 | tf_op jit(solution)/shard_map/all_to_all | solution.py:65
  77.8 33.7 %reduce-scatter.6.cloned.1.call-start = ((), (), s32[]{:S(2)}) async-start(), calls=%async_computation.7 | async-start | bytes 245760 | tf_op jit(solution)/shard_map/reduce_scatter | solution.py:55
  145.9 11.1 %copy-start.3 = (bf16[1,1,1024,256]{3,2,1,0:T(8,128)(2,1)S(1)}, bf16[1,1,1024,256]{3,2,1,0:T(8,128)(2,1)}, u32[]{:S(2)}) copy-start(bf16[1,1,1024,256]{3,2,1,0:T(8,128)(2,1)} %param.18) | copy-start | bytes 1572868
  145.9 11.0 %all-to-all-start.1 = ((f32[4,256,96]{1,2,0:T(8,128)}), f32[4,256,96]{1,2,0:T(8,128)S(1)}, u32[]{:S(2)}, u32[]{:S(2)}) async-start(f32[4,256,96]{1,2,0:T(8,128)} %copy.32), calls=%async_computation.3 | async-start | bytes 786432 | tf_op jit(solution)/shard_map/all_to_all | solution.py:65
  149.5 33.1 %reduce-scatter.8.cloned.1.call-start = ((), (), s32[]{:S(2)}) async-start(), calls=%async_computation.8 | async-start | bytes 245760 | tf_op jit(solution)/shard_map/reduce_scatter | solution.py:55
  215.9 12.3 %copy-start.4 = (bf16[1,1,1024,256]{3,2,1,0:T(8,128)(2,1)S(1)}, bf16[1,1,1024,256]{3,2,1,0:T(8,128)(2,1)}, u32[]{:S(2)}) copy-start(bf16[1,1,1024,256]{3,2,1,0:T(8,128)(2,1)} %param.18) | copy-start | bytes 1572868
  217.3 10.8 %all-to-all-start.2 = ((f32[4,256,96]{1,2,0:T(8,128)}), f32[4,256,96]{1,2,0:T(8,128)S(1)}, u32[]{:S(2)}, u32[]{:S(2)}) async-start(f32[4,256,96]{1,2,0:T(8,128)} %copy.37), calls=%async_computation.5 | async-start | bytes 786432 | tf_op jit(solution)/shard_map/all_to_all | solution.py:65
  232.1 0.9 copy-start
Sparse Core Ops, SparseCore 0:
  14.6 25.2 reduce-scatter.3
  86.1 25.3 reduce-scatter.5
  157.9 24.7 reduce-scatter.7
where the time goes:
time: 240 us
  blocking collectives  94.5 us (39%)
  waiting for transfers between devices  86.4 us (36%)
  between operations  26 us (11%)
  local copies, waits for them, and re-layouts  13 us (5%)
  starting transfers between devices  10.6 us (4%)
  other arithmetic  4.62 us (2%)
  matrix products  3.55 us (1%)
    all_gather x3, blocking collectives, advance(): gathered = lax.all_gather(share[None], 'blk', axis=0, tiled=True)  94.5 us
    reduce_scatter x3, waiting for transfers between devices, advance(): lax.psum_scatter(masked.astype(jnp.bfloat16), 'level', scatter_dimension=...  69 us
    all_to_all x3, waiting for transfers between devices, advance(): lax.all_to_all(sums, 'level', split_axis=0, concat_axis=2, tiled=True)  17.3 us
    all_to_all x3, starting transfers between devices, advance(): lax.all_to_all(sums, 'level', split_axis=0, concat_axis=2, tiled=True)  10.5 us
    dot_general x9, local copies, waits for them, and re-layouts, advance(): jnp.dot(dest_weights, gathered.reshape(blocks, -1), preferred_element_typ...  5.09 us
  transfers between devices with their start and end apart: 6, of which 6 were waited for; matrix products, arithmetic and copies ran while one was open for 0% of the time, Pallas kernels for 0%

commit v1 on v0

v1 whole, which is shorter than its diff:
```python
import functools

import jax
import jax.numpy as jnp
from jax import lax
from jax.experimental import pallas as pl
from jax.experimental.pallas import tpu as pltpu
from jax.sharding import Mesh, PartitionSpec as P


def x_size(mesh):
    blocks = mesh.shape["blk"]
    first = [getattr(d, "coords", None) for d in mesh.devices[0]]
    if any(c is None for c in first):
        return 2 if blocks % 2 == 0 else 1
    return len({c[0] for c in first})


def mid_kernel(step, zs, xs, order_ref, coup_ref, place_ref, *refs):
    my_z, my_x = place_ref[0], place_ref[1]
    pieces = [refs[h * zs : (h + 1) * zs] for h in range(step)]
    c0_ref = refs[step * zs]
    m_refs = refs[step * zs + 1 : step * zs + 1 + xs]
    inc_ref, out_ref = refs[-2:]
    group = order_ref[step]
    for mb in range(xs):
        xb = my_x ^ mb
        inc = mix(step, zs, xs, order_ref, coup_ref, pieces, group, my_z, xb)
        inc = inc.astype(jnp.bfloat16)
        inc_ref[xb] = inc
        delta = jnp.dot(inc, m_refs[mb][...], preferred_element_type=jnp.float32)
        out_ref[xb] = (c0_ref[group, xb].astype(jnp.float32) - delta).astype(jnp.bfloat16)


def mix(step, zs, xs, order_ref, coup_ref, pieces, group, my_z, xb):
    total = None
    for h in range(step):
        for m in range(zs):
            for xc in range(xs):
                w = coup_ref[group, my_z * xs + xb, order_ref[h] * (zs * xs) + (my_z ^ m) * xs + xc]
                term = w.astype(jnp.float32) * pieces[h][m][xc].astype(jnp.float32)
                total = term if total is None else total + term
    return total


def last_kernel(levels, zs, xs, order_ref, coup_ref, place_ref, *refs):
    my_z = place_ref[0]
    step = levels - 1
    pieces = [refs[h * zs : (h + 1) * zs] for h in range(step)]
    inc_refs = refs[step * zs : -1]
    out_ref = refs[-1]
    out_ref[order_ref[0]] = jnp.zeros(out_ref.shape[1:], out_ref.dtype)
    for h in range(1, step):
        out_ref[order_ref[h]] = inc_refs[h - 1][...]
    group = order_ref[step]
    for xb in range(xs):
        inc = mix(step, zs, xs, order_ref, coup_ref, pieces, group, my_z, xb)
        out_ref[group, xb] = inc.astype(jnp.bfloat16)


def per_device(zs, xs, sides, inverse, compress, expand, ranks, coupling, section_order):
    levels = lax.axis_size("level")
    blocks = zs * xs
    my_z, my_x = lax.axis_index("z"), lax.axis_index("x")
    sides, expand, basis = sides[0, 0], expand[0, 0], compress[0, 0]
    inverse = inverse[0, 0]
    subs, rows = inverse.shape[0], inverse.shape[1]
    rank_cap, width = basis.shape[1], sides.shape[1]
    cols = width // (levels * xs)
    tn = (((0,), (0,)), ((), ()))
    bf16, f32 = jnp.bfloat16, jnp.float32

    kept = jnp.arange(rank_cap, dtype=jnp.int32)[None, :] < ranks[0, 0]
    reduced = jnp.einsum(
        "jab,jak->jbk", inverse, basis.reshape(subs, rows, rank_cap), preferred_element_type=f32
    )
    reduced = jnp.where(kept, reduced.reshape(subs * rows, rank_cap), 0.0).astype(bf16)
    c0 = lax.dot_general(sides, reduced, tn, preferred_element_type=f32).astype(bf16)
    m_t = lax.dot_general(expand, reduced, tn, preferred_element_type=f32).astype(bf16)

    level_ids = jnp.arange(levels, dtype=jnp.int32)
    order = jnp.sum(
        jnp.where(section_order[None, :] == level_ids[:, None], level_ids[None, :], 0), axis=1
    ).astype(jnp.int32)
    place = jnp.stack([my_z, my_x]).astype(jnp.int32)
    coup = coupling.reshape(levels, blocks, levels * blocks)

    m_all = lax.all_gather(m_t, "level", axis=0)
    m_mid = jnp.stack(
        [lax.dynamic_index_in_dim(m_all, order[s], 0, keepdims=False) for s in range(1, levels - 1)]
    )
    m_parts = [m_mid] + [
        lax.ppermute(m_mid, "x", [(i, i ^ m) for i in range(xs)]) for m in range(1, xs)
    ]
    c0_all = lax.all_to_all(c0, ("level", "x"), 0, 0, tiled=True)
    c0_all = c0_all.reshape(levels, xs, cols, rank_cap)

    smem = pl.BlockSpec(memory_space=pltpu.SMEM)
    vmem = pl.BlockSpec(memory_space=pltpu.VMEM)
    share = jax.ShapeDtypeStruct((xs, cols, rank_cap), bf16)

    def exchange(part):
        return [part] + [
            lax.ppermute(part, "z", [(i, i ^ m) for i in range(zs)]) for m in range(1, zs)
        ]

    solved = lax.dynamic_index_in_dim(c0_all, order[0], 0, keepdims=False)
    pieces, incs = [], []
    for step in range(1, levels):
        pieces += exchange(solved)
        if step < levels - 1:
            ms = [part[step - 1] for part in m_parts]
            n_in = len(pieces) + 1 + len(ms)
            inc, solved = pl.pallas_call(
                functools.partial(mid_kernel, step, zs, xs),
                in_specs=[smem] * 3 + [vmem] * n_in,
                out_specs=[vmem, vmem],
                out_shape=[share, share],
                name=f"section_{step}",
            )(order, coup, place, *pieces, c0_all, *ms)
            incs.append(inc)
    inc_all = pl.pallas_call(
        functools.partial(last_kernel, levels, zs, xs),
        in_specs=[smem] * 3 + [vmem] * (len(pieces) + len(incs)),
        out_specs=vmem,
        out_shape=jax.ShapeDtypeStruct((levels, xs, cols, rank_cap), bf16),
        name="last_sums",
    )(order, coup, place, *pieces, *incs)
    inc = lax.all_to_all(
        inc_all.reshape(levels * xs * cols, rank_cap), ("level", "x"), 0, 0, tiled=True
    )

    update = lax.dot_general(expand, inc, (((1,), (1,)), ((), ())), preferred_element_type=f32)
    work = (sides.astype(f32) - update).astype(bf16).reshape(subs, rows, width)
    result = jnp.einsum("jab,jbr->jar", inverse, work, preferred_element_type=f32)
    return result.astype(bf16).reshape(1, 1, subs * rows, width)


def solution(mesh):
    levels, blocks = mesh.shape["level"], mesh.shape["blk"]
    xs = x_size(mesh)
    zs = blocks // xs
    split = Mesh(mesh.devices.reshape(levels, zs, xs), ("level", "z", "x"))
    seg = P("level", ("z", "x"))
    return jax.shard_map(
        functools.partial(per_device, zs, xs),
        mesh=split,
        in_specs=(seg, seg, seg, seg, seg, P(), P()),
        out_specs=seg,
        check_vma=False,
    )
```

time: 240 us -> 76.1 us (0.32)
  blocking collectives: 94.5 us -> 7.69 us
  waiting for transfers between devices: 86.4 us -> 14 us
  between operations: 26 us -> 6.25 us
  starting transfers between devices: 10.6 us -> 23.3 us
  Pallas kernels: 0 us -> 6.2 us
  other arithmetic: 4.62 us -> 0.75 us
  matrix products: 3.55 us -> 6.87 us
  local copies, waits for them, and re-layouts: 13 us -> 10.2 us
    all_gather x3 -> x1, blocking collectives: 94.5 us -> 7.69 us  [per_device(): m_all = lax.all_gather(m_t, 'level', axis=0)]
    reduce_scatter x3 -> x0, waiting for transfers between devices: 69 us -> none  [advance(): lax.psum_scatter(masked.astype(jnp.bfloat16), 'level', scatter_dimension=...]
    ppermute x0 -> x10, starting transfers between devices: none -> 14.8 us  [the longest x9 13.2 us: exchange(): lax.ppermute(part, 'z', [(i, i ^ m) for i in range(zs)])]
    all_to_all x3 -> x2, waiting for transfers between devices: 17.3 us -> 4.2 us  [the longest x1 4.2 us: per_device(): lax.all_to_all(inc_all.reshape(levels * xs * cols, rank_cap), ('level', '...]
    ppermute x0 -> x10, waiting for transfers between devices: none -> 9.78 us  [the longest x9 9.77 us: exchange(): lax.ppermute(part, 'z', [(i, i ^ m) for i in range(zs)])]
    pallas_call x0 -> x3, Pallas kernels: none -> 6.2 us  [the longest x2 4.16 us: per_device(): pl.pallas_call(functools.partial(mid_kernel, step, zs, xs), in_specs=[sme...]
    dot_general x9 -> x0, local copies, waits for them, and re-layouts: 5.09 us -> none  [advance(): jnp.dot(dest_weights, gathered.reshape(blocks, -1), preferred_element_typ...]
    dot_general x4, matrix products: 3.55 us -> 6.87 us  [the longest x1 3.14 us: per_device(): jnp.einsum('jab,jbr->jar', inverse, work, preferred_element_type=f32)]
  transfers between devices with their start and end apart: 6 -> 12, of which waited for: 6 -> 7; matrix products, arithmetic and copies ran while one was open for 0% -> 8% of each run, Pallas kernels for 0% -> 0%
where the time goes in v1:
time: 76.1 us; the launch traced here: 75.3 us
  starting transfers between devices  23.3 us (31%)
  waiting for transfers between devices  14 us (18%)
  local copies, waits for them, and re-layouts  10.2 us (13%)
  blocking collectives  7.69 us (10%)
  matrix products  6.87 us (9%)
  between operations  6.25 us (8%)
  Pallas kernels  6.2 us (8%)
    ppermute x9, starting transfers between devices, exchange(): lax.ppermute(part, 'z', [(i, i ^ m) for i in range(zs)])  13.2 us
    ppermute x9, waiting for transfers between devices, exchange(): lax.ppermute(part, 'z', [(i, i ^ m) for i in range(zs)])  9.77 us
    all_gather x1, blocking collectives, per_device(): m_all = lax.all_gather(m_t, 'level', axis=0)  7.69 us
    all_to_all x1, starting transfers between devices, per_device(): c0_all = lax.all_to_all(c0, ('level', 'x'), 0, 0, tiled=True)  5.19 us
    unnamed x41, local copies, waits for them, and re-layouts  4.89 us
    all_to_all x1, waiting for transfers between devices, per_device(): lax.all_to_all(inc_all.reshape(levels * xs * cols, rank_cap), ('level', '...  4.2 us
    pallas_call x2, Pallas kernels, per_device(): pl.pallas_call(functools.partial(mid_kernel, step, zs, xs), in_specs=[sme...  4.16 us
    all_to_all x1, starting transfers between devices, per_device(): lax.all_to_all(inc_all.reshape(levels * xs * cols, rank_cap), ('level', '...  3.39 us
  transfers between devices with their start and end apart: 12, of which 7 were waited for; matrix products, arithmetic and copies ran while one was open for 8% of the time, Pallas kernels for 0%

profile of v1, /device:TPU:0, one launch (start us, length us, event | category | flops | bytes accessed | tf_op | source)
XLA Modules:
  0.0 75.3 jit_solution(3128393329083754821)
XLA Ops:
  0.8 0.8 %copy-done = bf16[1,1,1,1024,1024]{4,3,2,1,0:T(8,128)(2,1)S(1)} copy-done((bf16[1,1,1,1024,1024]{4,3,2,1,0:T(8,128)(2,1)S(1)}, bf16[1,1,1,1024,1024]{4,3,2,1,0:T(8,128)(2,1)}, u32[]{:S(2)}) %copy-start) | copy-done | bytes 2097176
  1.6 1.9 %fusion.11 = bf16[1024,256]{1,0:T(8,128)(2,1)S(1)} fusion(bf16[1,1,1,1024,1024]{4,3,2,1,0:T(8,128)(2,1)S(1)} %copy-done, bf16[1,1,1024,256]{3,2,1,0:T(8,128)(2,1)} %param.9, pred[256]{0:T(512)(128)(4,1)S(1)} %iota_compare_fusion.1), kind=kOutput, calls=%fused_computation.8 | convolution fusion | flops 537395200 | bytes 3145984 | tf_op jit(solution)/shard_map/jab,jak->jbk/dot_general | solution.py:74
  3.5 0.8 %copy-done.19 = bf16[1024,256]{1,0:T(8,128)(2,1)} copy-done((bf16[1024,256]{1,0:T(8,128)(2,1)}, bf16[1024,256]{1,0:T(8,128)(2,1)S(1)}, u32[]{:S(2)}) %copy-start.19) | copy-done | bytes 524312
  4.8 0.8 %copy.15 = bf16[384,256]{1,0:T(8,128)(2,1)} copy(bf16[384,256]{0,1:T(8,128)(2,1)S(1)} %fusion.17) | data formatting | bytes 393216 | tf_op jit(solution)/shard_map/convert_element_type | solution.py:78
  5.6 5.2 %all-to-all-start = ((bf16[8,48,256]{2,1,0:T(8,128)(2,1)}), bf16[8,48,256]{2,1,0:T(8,128)(2,1)S(1)}, u32[]{:S(2)}, u32[]{:S(2)}) async-start(bf16[8,48,256]{2,1,0:T(8,128)(2,1)} %bitcast.7), calls=%async_computation | async-start | bytes 393216 | tf_op jit(solution)/shard_map/all_to_all | solution.py:95
  10.9 0.6 fusion.25
  13.9 1.4 %fusion.18 = bf16[256,256]{0,1:T(8,128)(2,1)S(1)} fusion(bf16[1024,256]{1,0:T(8,128)(2,1)} %copy-done.19, bf16[1,1,1024,256]{3,2,1,0:T(8,128)(2,1)S(1)} %copy-done.17), kind=kOutput, calls=%fused_computation.13 | convolution fusion | flops 134283264 | bytes 1179648 | tf_op jit(solution)/shard_map/dot_general | solution.py:79
  15.3 7.7 %all-gather = bf16[1024,256]{0,1:T(8,128)(2,1)S(1)} all-gather(bf16[256,256]{0,1:T(8,128)(2,1)S(1)} %fusion.18), channel_id=2, replica_groups=mesh['level'=4,'z'=4,'x'=2] {'level'}, dimensions={0}, use_global_device_ids=true | all-gather | bytes 655360 | tf_op jit(solution)/shard_map/all_gather | solution.py:88
  24.5 1.5 %collective-permute-start.3 = (bf16[2,256,256]{2,1,0:T(8,128)(2,1)S(1)}, bf16[2,256,256]{2,1,0:T(8,128)(2,1)S(1)}, u32[]{:S(2)}, u32[]{:S(2)}) collective-permute-start(bf16[2,256,256]{2,1,0:T(8,128)(2,1)S(1)} %pad_maximum_fusion), channel_id=1, source_target_pairs={{0,1},{1,0},{2,3},{3,2},{4,5},{5,4},{6,7},{7,6},{8,9},{9,8},{10,11... | collective-permute-start | bytes 786440 | tf_op jit(solution)/shard_map/ppermute | solution.py:93
  27.1 0.7 reshape.53.coup_ref
  28.4 0.6 pad_add_fusion.place_ref
  29.0 3.7 %collective-permute-start.2 = (bf16[2,48,256]{2,1,0:T(8,128)(2,1)S(1)}, bf16[2,48,256]{2,1,0:T(8,128)(2,1)S(1)}, u32[]{:S(2)}, u32[]{:S(2)}) collective-permute-start(bf16[2,48,256]{2,1,0:T(8,128)(2,1)S(1)} %dynamic-slice_bitcast_fusion.refs_0_), channel_id=1, source_target_pairs={{0,6},{2,4},{4,2},{6,0},{1,7},{3,5},{5,3},{7,1},{8,14},{10,12},{12... | collective-permute-start | bytes 147464 | tf_op jit(solution)/shard_map/ppermute | solution.py:104
  32.7 0.8 %collective-permute-start = (bf16[2,48,256]{2,1,0:T(8,128)(2,1)S(1)}, bf16[2,48,256]{2,1,0:T(8,128)(2,1)S(1)}, u32[]{:S(2)}, u32[]{:S(2)}) collective-permute-start(bf16[2,48,256]{2,1,0:T(8,128)(2,1)S(1)} %dynamic-slice_bitcast_fusion.refs_0_), channel_id=1, source_target_pairs={{0,2},{2,0},{4,6},{6,4},{1,3},{3,1},{5,7},{7,5},{8,10},{10,8},{12,... | collective-permute-start | bytes 147464 | tf_op jit(solution)/shard_map/ppermute | solution.py:104
  33.5 0.7 slice_bitcast_fusion
  34.2 0.8 %collective-permute-done.2.refs_3_ = bf16[2,48,256]{2,1,0:T(8,128)(2,1)S(1)} collective-permute-done((bf16[2,48,256]{2,1,0:T(8,128)(2,1)S(1)}, bf16[2,48,256]{2,1,0:T(8,128)(2,1)S(1)}, u32[]{:S(2)}, u32[]{:S(2)}) %collective-permute-start.2) | collective-permute-done | bytes 49184 | tf_op jit(solution)/shard_map/ppermute | solution.py:104
  35.0 2.7 %collective-permute-done.1.refs_2_ = bf16[2,48,256]{2,1,0:T(8,128)(2,1)S(1)} collective-permute-done((bf16[2,48,256]{2,1,0:T(8,128)(2,1)S(1)}, bf16[2,48,256]{2,1,0:T(8,128)(2,1)S(1)}, u32[]{:S(2)}, u32[]{:S(2)}) %collective-permute-start.1) | collective-permute-done | bytes 49184 | tf_op jit(solution)/shard_map/ppermute | solution.py:104
  38.3 2.0 %section_1.1 = (bf16[2,48,256]{2,1,0:T(8,128)(2,1)}, bf16[2,48,256]{2,1,0:T(8,128)(2,1)}) custom-call(s32[4]{0:T(128)} %copy-done.16, s32[4,8,32]{2,1,0:T(8,128)} %reshape.53.coup_ref, s32[2]{0:T(128)} %pad_add_fusion.place_ref, bf16[2,48,256]{2,1,0:T(8,128)(2,1)} %copy-done.5, bf16[2,48,256]{2,1,0:T(8,128)(2,1)} %copy-done.8, ...), custom_call_target="tpu_custom_call" | custom-call | tf_op jit(solution)/shard_map/section_1/pallas_call | solution.py:114
  40.3 2.1 %collective-permute-start.6 = (bf16[2,48,256]{2,1,0:T(8,128)(2,1)}, bf16[2,48,256]{2,1,0:T(8,128)(2,1)S(1)}, u32[]{:S(2)}, u32[]{:S(2)}) collective-permute-start(bf16[2,48,256]{2,1,0:T(8,128)(2,1)} %get-tuple-element.9.refs_4_), channel_id=1, source_target_pairs={{0,6},{2,4},{4,2},{6,0},{1,7},{3,5},{5,3},{7,1},{8,14},{10,12},{12... | collective-permute-start | bytes 147464 | tf_op jit(solution)/shard_map/ppermute | solution.py:104
  42.6 2.1 %collective-permute-start.4 = (bf16[2,48,256]{2,1,0:T(8,128)(2,1)}, bf16[2,48,256]{2,1,0:T(8,128)(2,1)S(1)}, u32[]{:S(2)}, u32[]{:S(2)}) collective-permute-start(bf16[2,48,256]{2,1,0:T(8,128)(2,1)} %get-tuple-element.9.refs_4_), channel_id=1, source_target_pairs={{0,2},{2,0},{4,6},{6,4},{1,3},{3,1},{5,7},{7,5},{8,10},{10,8},{12,... | collective-permute-start | bytes 147464 | tf_op jit(solution)/shard_map/ppermute | solution.py:104
  44.7 2.1 %collective-permute-done.6.refs_7_ = bf16[2,48,256]{2,1,0:T(8,128)(2,1)S(1)} collective-permute-done((bf16[2,48,256]{2,1,0:T(8,128)(2,1)}, bf16[2,48,256]{2,1,0:T(8,128)(2,1)S(1)}, u32[]{:S(2)}, u32[]{:S(2)}) %collective-permute-start.6) | collective-permute-done | bytes 49184 | tf_op jit(solution)/shard_map/ppermute | solution.py:104
  46.9 1.2 %collective-permute-done.5.refs_6_ = bf16[2,48,256]{2,1,0:T(8,128)(2,1)S(1)} collective-permute-done((bf16[2,48,256]{2,1,0:T(8,128)(2,1)}, bf16[2,48,256]{2,1,0:T(8,128)(2,1)S(1)}, u32[]{:S(2)}, u32[]{:S(2)}) %collective-permute-start.5) | collective-permute-done | bytes 49184 | tf_op jit(solution)/shard_map/ppermute | solution.py:104
  48.7 2.2 %section_2.1 = (bf16[2,48,256]{2,1,0:T(8,128)(2,1)}, bf16[2,48,256]{2,1,0:T(8,128)(2,1)}) custom-call(s32[4]{0:T(128)} %copy-done.16, s32[4,8,32]{2,1,0:T(8,128)} %reshape.53.coup_ref, s32[2]{0:T(128)} %pad_add_fusion.place_ref, bf16[2,48,256]{2,1,0:T(8,128)(2,1)} %copy-done.5, bf16[2,48,256]{2,1,0:T(8,128)(2,1)} %copy-done.8, ...), custom_call_target="tpu_custom_call" | custom-call | tf_op jit(solution)/shard_map/section_2/pallas_call | solution.py:114
  50.9 2.0 %collective-permute-start.9 = (bf16[2,48,256]{2,1,0:T(8,128)(2,1)}, bf16[2,48,256]{2,1,0:T(8,128)(2,1)S(1)}, u32[]{:S(2)}, u32[]{:S(2)}) collective-permute-start(bf16[2,48,256]{2,1,0:T(8,128)(2,1)} %get-tuple-element.10.refs_8_), channel_id=1, source_target_pairs={{0,6},{2,4},{4,2},{6,0},{1,7},{3,5},{5,3},{7,1},{8,14},{10,12},{12... | collective-permute-start | bytes 147464 | tf_op jit(solution)/shard_map/ppermute | solution.py:104
  53.3 2.0 %collective-permute-start.7 = (bf16[2,48,256]{2,1,0:T(8,128)(2,1)}, bf16[2,48,256]{2,1,0:T(8,128)(2,1)S(1)}, u32[]{:S(2)}, u32[]{:S(2)}) collective-permute-start(bf16[2,48,256]{2,1,0:T(8,128)(2,1)} %get-tuple-element.10.refs_8_), channel_id=1, source_target_pairs={{0,2},{2,0},{4,6},{6,4},{1,3},{3,1},{5,7},{7,5},{8,10},{10,8},{12,... | collective-permute-start | bytes 147464 | tf_op jit(solution)/shard_map/ppermute | solution.py:104
  55.3 1.7 %collective-permute-done.9.refs_11_ = bf16[2,48,256]{2,1,0:T(8,128)(2,1)S(1)} collective-permute-done((bf16[2,48,256]{2,1,0:T(8,128)(2,1)}, bf16[2,48,256]{2,1,0:T(8,128)(2,1)S(1)}, u32[]{:S(2)}, u32[]{:S(2)}) %collective-permute-start.9) | collective-permute-done | bytes 49184 | tf_op jit(solution)/shard_map/ppermute | solution.py:104
  57.0 1.2 %collective-permute-done.8.refs_10_ = bf16[2,48,256]{2,1,0:T(8,128)(2,1)S(1)} collective-permute-done((bf16[2,48,256]{2,1,0:T(8,128)(2,1)}, bf16[2,48,256]{2,1,0:T(8,128)(2,1)S(1)}, u32[]{:S(2)}, u32[]{:S(2)}) %collective-permute-start.8) | collective-permute-done | bytes 49184 | tf_op jit(solution)/shard_map/ppermute | solution.py:104
  58.8 2.0 %last_sums.1 = bf16[4,2,48,256]{3,2,1,0:T(8,128)(2,1)} custom-call(s32[4]{0:T(128)} %copy-done.16, s32[4,8,32]{2,1,0:T(8,128)} %reshape.53.coup_ref, s32[2]{0:T(128)} %pad_add_fusion.place_ref, bf16[2,48,256]{2,1,0:T(8,128)(2,1)} %copy-done.5, bf16[2,48,256]{2,1,0:T(8,128)(2,1)} %copy-done.8, bf16[2,48,256]{2,1,0:T(8,128)(2,1)} %copy-done.7, ...), custom_call_target="tpu_custom_call" | custom-call | tf_op jit(solution)/shard_map/last_sums/pallas_call | solution.py:122
  60.9 3.4 %all-to-all-start.1 = ((bf16[8,48,256]{2,1,0:T(8,128)(2,1)}), bf16[8,48,256]{2,1,0:T(8,128)(2,1)S(1)}, u32[]{:S(2)}, u32[]{:S(2)}) async-start(bf16[8,48,256]{2,1,0:T(8,128)(2,1)} %bitcast.73), calls=%async_computation.1 | async-start | bytes 393216 | tf_op jit(solution)/shard_map/all_to_all | solution.py:129
  64.3 1.4 %copy.14 = bf16[1,1,1024,384]{2,3,1,0:T(8,128)(2,1)S(1)} copy(bf16[1,1,1024,384]{3,2,1,0:T(8,128)(2,1)} %param.7) | data formatting | bytes 1572864 | tf_op args[0]
  65.7 4.2 %all-to-all-done.1 = bf16[8,48,256]{2,1,0:T(8,128)(2,1)S(1)} async-done(((bf16[8,48,256]{2,1,0:T(8,128)(2,1)}), bf16[8,48,256]{2,1,0:T(8,128)(2,1)S(1)}, u32[]{:S(2)}, u32[]{:S(2)}) %all-to-all-start.1) | async-done | bytes 196640 | tf_op jit(solution)/shard_map/all_to_all | solution.py:129
  69.9 3.1 %fusion.14 = bf16[1,1,1024,384]{2,3,1,0:T(8,128)(2,1)} fusion(bf16[1,1,1,1024,1024]{4,3,2,1,0:T(8,128)(2,1)S(1)} %copy-done, bf16[384,256]{1,0:T(8,128)(2,1)S(1)} %bitcast.74, bf16[1,1,1024,384]{2,3,1,0:T(8,128)(2,1)S(1)} %copy.14, bf16[1,1,1024,256]{3,2,1,0:T(8,128)(2,1)} %param.10), kind=kOutput, calls=%fused_computation.9 | convolution fusion | flops 1008205824 | bytes 4390912 | tf_op jit(solution)/shard_map/jab,jbr->jar/dot_general | solution.py:135
  73.0 2.3 %copy.17 = bf16[1,1,1024,384]{3,2,1,0:T(8,128)(2,1)} copy(bf16[1,1,1024,384]{2,3,1,0:T(8,128)(2,1)} %fusion.14) | data formatting | bytes 1572864 | tf_op jit(solution)/shard_map/reshape | solution.py:136
  (53 shorter events, 3.3 us)
Async XLA Ops:
  0.0 1.6 %copy-start = (bf16[1,1,1,1024,1024]{4,3,2,1,0:T(8,128)(2,1)S(1)}, bf16[1,1,1,1024,1024]{4,3,2,1,0:T(8,128)(2,1)}, u32[]{:S(2)}) copy-start(bf16[1,1,1,1024,1024]{4,3,2,1,0:T(8,128)(2,1)} %param.8) | copy-start | bytes 6291460
  1.6 2.7 %copy-start.4 = (bf16[1,1,1024,384]{3,2,1,0:T(8,128)(2,1)S(1)}, bf16[1,1,1024,384]{3,2,1,0:T(8,128)(2,1)}, u32[]{:S(2)}) copy-start(bf16[1,1,1024,384]{3,2,1,0:T(8,128)(2,1)} %param.7) | copy-start | bytes 2359300
  3.5 0.8 %copy-start.19 = (bf16[1024,256]{1,0:T(8,128)(2,1)}, bf16[1024,256]{1,0:T(8,128)(2,1)S(1)}, u32[]{:S(2)}) copy-start(bf16[1024,256]{1,0:T(8,128)(2,1)S(1)} %fusion.11) | copy-start | bytes 1572868
  4.3 6.5 %copy-start.18 = (s32[4]{0:T(128)S(1)}, s32[4]{0:T(128)}, u32[]{:S(2)}) copy-start(s32[4]{0:T(128)} %param.13) | copy-start | bytes 52
  4.3 9.6 %copy-start.17 = (bf16[1,1,1024,256]{3,2,1,0:T(8,128)(2,1)S(1)}, bf16[1,1,1024,256]{3,2,1,0:T(8,128)(2,1)}, u32[]{:S(2)}) copy-start(bf16[1,1,1024,256]{3,2,1,0:T(8,128)(2,1)} %param.10) | copy-start | bytes 1572868
  5.6 23.4 %all-to-all-start = ((bf16[8,48,256]{2,1,0:T(8,128)(2,1)}), bf16[8,48,256]{2,1,0:T(8,128)(2,1)S(1)}, u32[]{:S(2)}, u32[]{:S(2)}) async-start(bf16[8,48,256]{2,1,0:T(8,128)(2,1)} %bitcast.7), calls=%async_computation | async-start | bytes 393216 | tf_op jit(solution)/shard_map/all_to_all | solution.py:95
  10.8 16.3 %copy-start.12 = (s32[4,8,4,8]{3,2,1,0:T(4,128)S(1)}, s32[4,8,4,8]{3,2,1,0:T(4,128)}, u32[]{:S(2)}) copy-start(s32[4,8,4,8]{3,2,1,0:T(4,128)} %param.12) | copy-start | bytes 12292
  10.9 16.9 %copy-start.16 = (s32[4]{0:T(128)}, s32[4]{0:T(128)S(1)}, u32[]{:S(2)}) copy-start(s32[4]{0:T(128)S(1)} %select_reduce_fusion.order_ref) | copy-start | bytes 52
  24.4 13.3 %copy-start.3 = (bf16[1,256,256]{2,1,0:T(8,128)(2,1)}, bf16[1,256,256]{2,1,0:T(8,128)(2,1)S(1)}, u32[]{:S(2)}) copy-start(bf16[1,256,256]{2,1,0:T(8,128)(2,1)S(1)} %get-tuple-element.14) | copy-start | bytes 393220
  24.4 23.6 %copy-start.2 = (bf16[1,256,256]{2,1,0:T(8,128)(2,1)}, bf16[1,256,256]{2,1,0:T(8,128)(2,1)S(1)}, u32[]{:S(2)}) copy-start(bf16[1,256,256]{2,1,0:T(8,128)(2,1)S(1)} %get-tuple-element.13) | copy-start | bytes 393220
  24.5 9.0 %collective-permute-start.3 = (bf16[2,256,256]{2,1,0:T(8,128)(2,1)S(1)}, bf16[2,256,256]{2,1,0:T(8,128)(2,1)S(1)}, u32[]{:S(2)}, u32[]{:S(2)}) collective-permute-start(bf16[2,256,256]{2,1,0:T(8,128)(2,1)S(1)} %pad_maximum_fusion), channel_id=1, source_target_pairs={{0,1},{1,0},{2,3},{3,2},{4,5},{5,4},{6,7},{7,6},{8,9},{9,8},{10,11... | collective-permute-start | bytes 786440 | tf_op jit(solution)/shard_map/ppermute | solution.py:93
  29.0 8.7 %copy-start.1 = (bf16[8,48,256]{2,1,0:T(8,128)(2,1)}, bf16[8,48,256]{2,1,0:T(8,128)(2,1)S(1)}, u32[]{:S(2)}) copy-start(bf16[8,48,256]{2,1,0:T(8,128)(2,1)S(1)} %all-to-all-done) | copy-start | bytes 589828
  29.0 8.7 %copy-start.5 = (bf16[2,48,256]{2,1,0:T(8,128)(2,1)}, bf16[2,48,256]{2,1,0:T(8,128)(2,1)S(1)}, u32[]{:S(2)}) copy-start(bf16[2,48,256]{2,1,0:T(8,128)(2,1)S(1)} %dynamic-slice_bitcast_fusion.refs_0_) | copy-start | bytes 147460
  29.0 6.0 %collective-permute-start.2 = (bf16[2,48,256]{2,1,0:T(8,128)(2,1)S(1)}, bf16[2,48,256]{2,1,0:T(8,128)(2,1)S(1)}, u32[]{:S(2)}, u32[]{:S(2)}) collective-permute-start(bf16[2,48,256]{2,1,0:T(8,128)(2,1)S(1)} %dynamic-slice_bitcast_fusion.refs_0_), channel_id=1, source_target_pairs={{0,6},{2,4},{4,2},{6,0},{1,7},{3,5},{5,3},{7,1},{8,14},{10,12},{12... | collective-permute-start | bytes 147464 | tf_op jit(solution)/shard_map/ppermute | solution.py:104
  32.7 5.0 %collective-permute-start.1 = (bf16[2,48,256]{2,1,0:T(8,128)(2,1)S(1)}, bf16[2,48,256]{2,1,0:T(8,128)(2,1)S(1)}, u32[]{:S(2)}, u32[]{:S(2)}) collective-permute-start(bf16[2,48,256]{2,1,0:T(8,128)(2,1)S(1)} %dynamic-slice_bitcast_fusion.refs_0_), channel_id=1, source_target_pairs={{0,4},{2,6},{4,0},{6,2},{1,5},{3,7},{5,1},{7,3},{8,12},{10,14},{12... | collective-permute-start | bytes 147464 | tf_op jit(solution)/shard_map/ppermute | solution.py:104
  32.7 5.0 %collective-permute-start = (bf16[2,48,256]{2,1,0:T(8,128)(2,1)S(1)}, bf16[2,48,256]{2,1,0:T(8,128)(2,1)S(1)}, u32[]{:S(2)}, u32[]{:S(2)}) collective-permute-start(bf16[2,48,256]{2,1,0:T(8,128)(2,1)S(1)} %dynamic-slice_bitcast_fusion.refs_0_), channel_id=1, source_target_pairs={{0,2},{2,0},{4,6},{6,4},{1,3},{3,1},{5,7},{7,5},{8,10},{10,8},{12,... | collective-permute-start | bytes 147464 | tf_op jit(solution)/shard_map/ppermute | solution.py:104
  35.0 2.7 %copy-start.6 = (bf16[2,48,256]{2,1,0:T(8,128)(2,1)}, bf16[2,48,256]{2,1,0:T(8,128)(2,1)S(1)}, u32[]{:S(2)}) copy-start(bf16[2,48,256]{2,1,0:T(8,128)(2,1)S(1)} %collective-permute-done.2.refs_3_) | copy-start | bytes 147460
  37.7 0.6 copy-start.7
  37.7 0.6 copy-start.8
  40.3 6.5 %collective-permute-start.6 = (bf16[2,48,256]{2,1,0:T(8,128)(2,1)}, bf16[2,48,256]{2,1,0:T(8,128)(2,1)S(1)}, u32[]{:S(2)}, u32[]{:S(2)}) collective-permute-start(bf16[2,48,256]{2,1,0:T(8,128)(2,1)} %get-tuple-element.9.refs_4_), channel_id=1, source_target_pairs={{0,6},{2,4},{4,2},{6,0},{1,7},{3,5},{5,3},{7,1},{8,14},{10,12},{12... | collective-permute-start | bytes 147464 | tf_op jit(solution)/shard_map/ppermute | solution.py:104
  42.5 5.6 %collective-permute-start.5 = (bf16[2,48,256]{2,1,0:T(8,128)(2,1)}, bf16[2,48,256]{2,1,0:T(8,128)(2,1)S(1)}, u32[]{:S(2)}, u32[]{:S(2)}) collective-permute-start(bf16[2,48,256]{2,1,0:T(8,128)(2,1)} %get-tuple-element.9.refs_4_), channel_id=1, source_target_pairs={{0,4},{2,6},{4,0},{6,2},{1,5},{3,7},{5,1},{7,3},{8,12},{10,14},{12... | collective-permute-start | bytes 147464 | tf_op jit(solution)/shard_map/ppermute | solution.py:104
  42.6 5.5 %collective-permute-start.4 = (bf16[2,48,256]{2,1,0:T(8,128)(2,1)}, bf16[2,48,256]{2,1,0:T(8,128)(2,1)S(1)}, u32[]{:S(2)}, u32[]{:S(2)}) collective-permute-start(bf16[2,48,256]{2,1,0:T(8,128)(2,1)} %get-tuple-element.9.refs_4_), channel_id=1, source_target_pairs={{0,2},{2,0},{4,6},{6,4},{1,3},{3,1},{5,7},{7,5},{8,10},{10,8},{12,... | collective-permute-start | bytes 147464 | tf_op jit(solution)/shard_map/ppermute | solution.py:104
  46.9 1.2 %copy-start.9 = (bf16[2,48,256]{2,1,0:T(8,128)(2,1)}, bf16[2,48,256]{2,1,0:T(8,128)(2,1)S(1)}, u32[]{:S(2)}) copy-start(bf16[2,48,256]{2,1,0:T(8,128)(2,1)S(1)} %collective-permute-done.6.refs_7_) | copy-start | bytes 147460
  48.1 0.6 copy-start.10
  48.1 0.6 copy-start.11
  50.9 6.1 %collective-permute-start.9 = (bf16[2,48,256]{2,1,0:T(8,128)(2,1)}, bf16[2,48,256]{2,1,0:T(8,128)(2,1)S(1)}, u32[]{:S(2)}, u32[]{:S(2)}) collective-permute-start(bf16[2,48,256]{2,1,0:T(8,128)(2,1)} %get-tuple-element.10.refs_8_), channel_id=1, source_target_pairs={{0,6},{2,4},{4,2},{6,0},{1,7},{3,5},{5,3},{7,1},{8,14},{10,12},{12... | collective-permute-start | bytes 147464 | tf_op jit(solution)/shard_map/ppermute | solution.py:104
  52.8 5.4 %collective-permute-start.8 = (bf16[2,48,256]{2,1,0:T(8,128)(2,1)}, bf16[2,48,256]{2,1,0:T(8,128)(2,1)S(1)}, u32[]{:S(2)}, u32[]{:S(2)}) collective-permute-start(bf16[2,48,256]{2,1,0:T(8,128)(2,1)} %get-tuple-element.10.refs_8_), channel_id=1, source_target_pairs={{0,4},{2,6},{4,0},{6,2},{1,5},{3,7},{5,1},{7,3},{8,12},{10,14},{12... | collective-permute-start | bytes 147464 | tf_op jit(solution)/shard_map/ppermute | solution.py:104
  53.3 5.0 %collective-permute-start.7 = (bf16[2,48,256]{2,1,0:T(8,128)(2,1)}, bf16[2,48,256]{2,1,0:T(8,128)(2,1)S(1)}, u32[]{:S(2)}, u32[]{:S(2)}) collective-permute-start(bf16[2,48,256]{2,1,0:T(8,128)(2,1)} %get-tuple-element.10.refs_8_), channel_id=1, source_target_pairs={{0,2},{2,0},{4,6},{6,4},{1,3},{3,1},{5,7},{7,5},{8,10},{10,8},{12,... | collective-permute-start | bytes 147464 | tf_op jit(solution)/shard_map/ppermute | solution.py:104
  57.0 1.2 %copy-start.13 = (bf16[2,48,256]{2,1,0:T(8,128)(2,1)}, bf16[2,48,256]{2,1,0:T(8,128)(2,1)S(1)}, u32[]{:S(2)}) copy-start(bf16[2,48,256]{2,1,0:T(8,128)(2,1)S(1)} %collective-permute-done.9.refs_11_) | copy-start | bytes 147460
  58.2 0.6 copy-start.14
  58.2 0.6 copy-start.15
  60.9 9.0 %all-to-all-start.1 = ((bf16[8,48,256]{2,1,0:T(8,128)(2,1)}), bf16[8,48,256]{2,1,0:T(8,128)(2,1)S(1)}, u32[]{:S(2)}, u32[]{:S(2)}) async-start(bf16[8,48,256]{2,1,0:T(8,128)(2,1)} %bitcast.73), calls=%async_computation.1 | async-start | bytes 393216 | tf_op jit(solution)/shard_map/all_to_all | solution.py:129

commit v2 on v1

v2 whole, which is shorter than its diff:
```python
import functools

import jax
import jax.numpy as jnp
from jax import lax
from jax.experimental import pallas as pl
from jax.experimental.pallas import tpu as pltpu
from jax.sharding import Mesh, PartitionSpec as P

BF16, F32 = jnp.bfloat16, jnp.float32
NN = (((1,), (0,)), ((), ()))
NT = (((1,), (1,)), ((), ()))
TN = (((0,), (0,)), ((), ()))
MIB = 1 << 20


def dot(a, b, dims):
    return lax.dot_general(a, b, dims, preferred_element_type=F32)


def x_size(mesh):
    blocks = mesh.shape["blk"]
    coords = [getattr(d, "coords", None) for d in mesh.devices[0]]
    if any(c is None for c in coords):
        return 2 if blocks % 2 == 0 else 1
    return len({c[0] for c in coords})


def call(kernel, outs, name, flops, nbytes, vmem, **kw):
    return pl.pallas_call(
        kernel,
        out_shape=outs,
        name=name,
        cost_estimate=pl.CostEstimate(flops=flops, bytes_accessed=nbytes, transcendentals=0),
        compiler_params=pltpu.CompilerParams(vmem_limit_bytes=vmem),
        **kw,
    )


def prep_kernel(chunk, rank_ref, c_hbm, d_hbm, r_hbm, e_hbm, out_ref, c, d, r, e, acc, sems):
    subs, rows = d_hbm.shape[0], d_hbm.shape[1]
    parts = rows // chunk
    copies = [pltpu.make_async_copy(c_hbm, c, sems.at[0])]
    for j in range(subs):
        for i in range(parts):
            at = pl.ds(i * chunk, chunk)
            copies.append(
                pltpu.make_async_copy(d_hbm.at[j, at], d.at[j, at], sems.at[1 + j * parts + i])
            )
    copies.append(pltpu.make_async_copy(r_hbm, r, sems.at[1 + subs * parts]))
    copies.append(pltpu.make_async_copy(e_hbm, e, sems.at[2 + subs * parts]))
    for copy in copies:
        copy.start()
    copies[0].wait()
    for j in range(subs):
        wide = pl.ds(j * rows, rows)
        for i in range(parts):
            copies[1 + j * parts + i].wait()
            part = dot(
                c[pl.ds(j * rows + i * chunk, chunk), :], d[j, pl.ds(i * chunk, chunk), :], TN
            )
            acc[:, wide] = part if i == 0 else acc[:, wide] + part
    a = acc[...].astype(BF16)
    kept = lax.broadcasted_iota(jnp.int32, (a.shape[0], 1), 0) < rank_ref[0, 0]
    copies[-2].wait()
    c0 = jnp.where(kept, dot(a, r[...], NN), 0.0).T.astype(BF16)
    copies[-1].wait()
    m = jnp.where(kept, dot(a, e[...], NN), 0.0).astype(BF16)
    levels, xs = out_ref.shape[0], out_ref.shape[1]
    cols, half = c0.shape[0] // (levels * xs), m.shape[0] // 2
    for level in range(levels):
        for x in range(xs):
            at = (level * xs + x) * cols
            out_ref[level, x, :cols] = c0[at : at + cols]
            out_ref[level, x, cols:] = m[level % 2 * half : (level % 2 + 1) * half]


def weights_kernel(zs, xs, levels, order_ref, coup_ref, w_ref, pick_ref):
    my_z = lax.axis_index("z")
    blocks = zs * xs
    row = 0
    for step in range(1, levels):
        for xb in range(xs):
            for h in range(step):
                for m in range(zs):
                    for xc in range(xs):
                        at = order_ref[h] * blocks + (my_z ^ m) * xs + xc
                        w = coup_ref[order_ref[step], my_z * xs + xb, at].astype(F32)
                        w_ref[pl.ds(row, 1), :] = jnp.full((1, w_ref.shape[1]), w, F32)
                        row += 1
    for step in range(levels):
        for g in range(levels):
            hit = (order_ref[step] == g).astype(F32)
            pick_ref[pl.ds(step * levels + g, 1), :] = jnp.full((1, w_ref.shape[1]), hit, F32)


def mix(first, step, zs, xs, w_ref, pieces, xb):
    row = first + xb * step * zs * xs
    total = None
    for h in range(step):
        for m in range(zs):
            for xc in range(xs):
                term = w_ref[pl.ds(row, 1), :] * pieces[h * zs + m][xc].astype(F32)
                total = term if total is None else total + term
                row += 1
    return total


def first_row(step, zs, xs):
    return xs * zs * xs * (step * (step - 1) // 2)


def mid_kernel(step, zs, xs, *refs):
    pieces = refs[: step * zs]
    w_ref, c0_ref, own_ref, other_ref, inc_ref, out_ref = refs[step * zs :]
    half = own_ref.shape[1]
    core = lax.rem(lax.axis_index("level"), 2)
    mine = pl.ds(pl.multiple_of(core * half, half), half)
    theirs = pl.ds(pl.multiple_of((1 - core) * half, half), half)
    for xb in range(xs):
        inc = mix(first_row(step, zs, xs), step, zs, xs, w_ref, pieces, xb).astype(BF16)
        inc_ref[xb] = inc
        out_ref[xb, :, mine] = (
            c0_ref[xb, :, mine].astype(F32) - dot(inc, own_ref[xb], NT)
        ).astype(BF16)
        out_ref[xb, :, theirs] = (
            c0_ref[xb, :, theirs].astype(F32) - dot(inc, other_ref[xb], NT)
        ).astype(BF16)


def last_kernel(levels, zs, xs, *refs):
    step = levels - 1
    pieces = refs[: step * zs]
    w_ref, pick_ref = refs[step * zs : step * zs + 2]
    inc_refs = refs[step * zs + 2 : -1]
    out_ref = refs[-1]
    for xb in range(xs):
        incs = [ref[xb].astype(F32) for ref in inc_refs]
        incs.append(mix(first_row(step, zs, xs), step, zs, xs, w_ref, pieces, xb))
        for g in range(levels):
            total = None
            for h in range(1, levels):
                term = pick_ref[pl.ds(h * levels + g, 1), :] * incs[h - 1]
                total = term if total is None else total + term
            out_ref[g, xb] = total.astype(BF16)


def full_kernel(d_hbm, r_hbm, e_hbm, dr_ref, de_ref, d, r, e, sems):
    copies = [
        pltpu.make_async_copy(r_hbm, r, sems.at[0]),
        pltpu.make_async_copy(e_hbm, e, sems.at[1]),
        pltpu.make_async_copy(d_hbm, d, sems.at[2]),
    ]
    for copy in copies:
        copy.start()
    for copy in copies:
        copy.wait()
    for j in range(d.shape[0]):
        at = pl.ds(j * d.shape[1], d.shape[1])
        dr_ref[at, :] = dot(d[j], r[at, :], NN)
        de_ref[at, :] = dot(d[j], e[at, :], NN).astype(BF16)


def final_kernel(tiles, inc_ref, dr_ref, de_ref, out_hbm, out, sems):
    tile = out.shape[0] // tiles
    copies = []
    for t in range(tiles):
        at = pl.ds(t * tile, tile)
        out[at, :] = (dr_ref[at, :] - dot(de_ref[at, :], inc_ref[...], NT)).astype(BF16)
        copies.append(pltpu.make_async_copy(out.at[at], out_hbm.at[at], sems.at[t]))
        copies[-1].start()
    for copy in copies:
        copy.wait()


def per_device(zs, xs, sides, inverse, compress, expand, ranks, coupling, section_order):
    levels = lax.axis_size("level")
    blocks = zs * xs
    sides, expand, basis, inverse = sides[0, 0], expand[0, 0], compress[0, 0], inverse[0, 0]
    subs, rows = inverse.shape[0], inverse.shape[1]
    seg, width = sides.shape
    rank_cap = basis.shape[1]
    cols = width // (levels * xs)
    half = rank_cap // 2
    smem = pl.BlockSpec(memory_space=pltpu.SMEM)
    vmem = pl.BlockSpec(memory_space=pltpu.VMEM)
    hbm = pl.BlockSpec(memory_space=pl.ANY)
    shape = jax.ShapeDtypeStruct

    chunk = rows // 4 if rows % 512 == 0 else rows
    n_copies = 3 + subs * (rows // chunk)
    payload = call(
        functools.partial(prep_kernel, chunk),
        shape((levels, xs, cols + half, rank_cap), BF16),
        "prep",
        2 * rank_cap * (seg * rows + seg * (width + rank_cap)),
        2 * (seg * (rows + width + 2 * rank_cap)),
        62 * MIB,
        in_specs=[smem] + [hbm] * 4,
        out_specs=vmem,
        scratch_shapes=[
            pltpu.VMEM(basis.shape, BF16),
            pltpu.VMEM(inverse.shape, BF16),
            pltpu.VMEM(sides.shape, BF16),
            pltpu.VMEM(expand.shape, BF16),
            pltpu.VMEM((rank_cap, seg), F32),
            pltpu.SemaphoreType.DMA((n_copies,)),
        ],
    )(ranks, basis, inverse, sides, expand)

    level_ids = jnp.arange(levels, dtype=jnp.int32)
    order = jnp.sum(
        jnp.where(section_order[None, :] == level_ids[:, None], level_ids[None, :], 0), axis=1
    ).astype(jnp.int32)

    shares = lax.all_to_all(
        payload.reshape(levels * xs * (cols + half), rank_cap), ("level", "x"), 0, 0, tiled=True
    ).reshape(levels, xs, cols + half, rank_cap)

    n_rows = first_row(levels, zs, xs)
    w_rows, picks = call(
        functools.partial(weights_kernel, zs, xs, levels),
        (shape((n_rows, rank_cap), F32), shape((levels * levels, rank_cap), F32)),
        "weights",
        1 << 20,
        4 * n_rows * rank_cap,
        4 * MIB,
        in_specs=[smem, smem],
        out_specs=(vmem, vmem),
    )(order, coupling.reshape(levels, blocks, levels * blocks))

    dr, de = call(
        full_kernel,
        (shape((seg, width), F32), shape((seg, rank_cap), BF16)),
        "full",
        2 * seg * rows * (width + rank_cap),
        2 * seg * (rows + 3 * width + 2 * rank_cap),
        62 * MIB,
        in_specs=[hbm] * 3,
        out_specs=(vmem, vmem),
        scratch_shapes=[
            pltpu.VMEM(inverse.shape, BF16),
            pltpu.VMEM(sides.shape, BF16),
            pltpu.VMEM(expand.shape, BF16),
            pltpu.SemaphoreType.DMA((3,)),
        ],
    )(inverse, sides, expand)

    shares, w_rows, picks, dr, de = lax.optimization_barrier((shares, w_rows, picks, dr, de))

    def part_of(step, start, size):
        zero = jnp.zeros((), jnp.int32)
        at = (order[step], zero, jnp.full((), start, jnp.int32), zero)
        return lax.dynamic_slice(shares, at, (1, xs, size, rank_cap))

    m_mine = jnp.concatenate([part_of(s, cols, half) for s in range(1, levels - 1)])
    m_other = lax.ppermute(m_mine, "level", [(i, i ^ 1) for i in range(levels)])

    def exchange(part):
        return [part] + [
            lax.ppermute(part, "z", [(i, i ^ m) for i in range(zs)]) for m in range(1, zs)
        ]

    share = shape((xs, cols, rank_cap), BF16)
    size = 2 * xs * cols * rank_cap
    solved = part_of(0, 0, cols)[0]
    pieces, incs = [], []
    for step in range(1, levels):
        pieces += exchange(solved)
        flops = 2 * step * zs * xs * size
        if step < levels - 1:
            inc, solved = call(
                functools.partial(mid_kernel, step, zs, xs),
                (share, share),
                f"section_{step}",
                flops,
                len(pieces) * size,
                4 * MIB,
                in_specs=[vmem] * (len(pieces) + 4),
                out_specs=(vmem, vmem),
            )(*pieces, w_rows, part_of(step, 0, cols)[0], m_mine[step - 1], m_other[step - 1])
            incs.append(inc)
    inc_all = call(
        functools.partial(last_kernel, levels, zs, xs),
        shape((levels, xs, cols, rank_cap), BF16),
        "last_sums",
        flops,
        len(pieces) * size,
        4 * MIB,
        in_specs=[vmem] * (len(pieces) + 2 + len(incs)),
        out_specs=vmem,
    )(*pieces, w_rows, picks, *incs)
    inc = lax.all_to_all(
        inc_all.reshape(levels * xs * cols, rank_cap), ("level", "x"), 0, 0, tiled=True
    )

    tiles = 4 if seg % 64 == 0 else 1
    result = call(
        functools.partial(final_kernel, tiles),
        shape((seg, width), BF16),
        "final",
        2 * seg * rank_cap * width,
        seg * (6 * width + 2 * rank_cap),
        16 * MIB,
        in_specs=[vmem] * 3,
        out_specs=hbm,
        scratch_shapes=[pltpu.VMEM((seg, width), BF16), pltpu.SemaphoreType.DMA((tiles,))],
    )(inc, dr, de)
    return result[None, None]


def solution(mesh):
    levels, blocks = mesh.shape["level"], mesh.shape["blk"]
    xs = x_size(mesh)
    zs = blocks // xs
    split = Mesh(mesh.devices.reshape(levels, zs, xs), ("level", "z", "x"))
    seg = P("level", ("z", "x"))
    return jax.shard_map(
        functools.partial(per_device, zs, xs),
        mesh=split,
        in_specs=(seg, seg, seg, seg, seg, P(), P()),
        out_specs=seg,
        check_vma=False,
    )
```

time: 76.1 us -> 59.7 us (0.78)
  local copies, waits for them, and re-layouts: 10.2 us -> 0.82 us
  matrix products: 6.87 us -> 0 us
  Pallas kernels: 6.2 us -> 12.4 us
  starting transfers between devices: 23.3 us -> 18.7 us
  waiting for transfers between devices: 14 us -> 11 us
  blocking collectives: 7.69 us -> 9.24 us
    all_to_all x0 -> x1, blocking collectives: none -> 9.24 us  [per_device(): lax.all_to_all(inc_all.reshape(levels * xs * cols, rank_cap), ('level', '...]
    all_gather x1 -> x0, blocking collectives: 7.69 us -> none  [per_device(): m_all = lax.all_gather(m_t, 'level', axis=0)]
    dot_general x4 -> x0, matrix products: 6.87 us -> none  [the longest x1 3.14 us: per_device(): jnp.einsum('jab,jbr->jar', inverse, work, preferred_element_type=f32)]
    pallas_call x3 -> x7, Pallas kernels: 6.2 us -> 12.4 us  [the longest x1 5.16 us: per_device(): call(full_kernel, (shape((seg, width), F32), shape((seg, rank_cap), BF16)...]
    unnamed x41 -> x8, local copies, waits for them, and re-layouts: 4.89 us -> 0.02 us
    all_to_all x2 -> x1, waiting for transfers between devices: 4.2 us -> 0.35 us  [per_device(): lax.all_to_all(payload.reshape(levels * xs * (cols + half), rank_cap), ('...]
    all_to_all x2 -> x1, starting transfers between devices: 8.59 us -> 5.21 us  [per_device(): lax.all_to_all(payload.reshape(levels * xs * (cols + half), rank_cap), ('...]
    reshape x2 -> x1, local copies, waits for them, and re-layouts: 2.98 us -> 0.09 us  [per_device(): coupling.reshape(levels, blocks, levels * blocks)]
  transfers between devices with their start and end apart: 12 -> 11, of which waited for: 7 -> 7; matrix products, arithmetic and copies ran while one was open for 8% -> 2% of each run, Pallas kernels for 0% -> 10%
where the time goes in v2:
time: 59.7 us; the launch traced here: 59.4 us
  starting transfers between devices  18.7 us (31%)
  Pallas kernels  12.4 us (21%)
  waiting for transfers between devices  11 us (18%)
  blocking collectives  9.24 us (15%)
  between operations  6.4 us (11%)
  other arithmetic  0.84 us (1%)
  local copies, waits for them, and re-layouts  0.82 us (1%)
    ppermute x9, starting transfers between devices, exchange(): lax.ppermute(part, 'z', [(i, i ^ m) for i in range(zs)])  13.3 us
    ppermute x9, waiting for transfers between devices, exchange(): lax.ppermute(part, 'z', [(i, i ^ m) for i in range(zs)])  10.6 us
    all_to_all x1, blocking collectives, per_device(): lax.all_to_all(inc_all.reshape(levels * xs * cols, rank_cap), ('level', '...  9.24 us
    all_to_all x1, starting transfers between devices, per_device(): lax.all_to_all(payload.reshape(levels * xs * (cols + half), rank_cap), ('...  5.21 us
    pallas_call x1, Pallas kernels, per_device(): call(full_kernel, (shape((seg, width), F32), shape((seg, rank_cap), BF16)...  5.16 us
    pallas_call x1, Pallas kernels, per_device(): call(functools.partial(prep_kernel, chunk), shape((levels, xs, cols + hal...  4.19 us
  transfers between devices with their start and end apart: 11, of which 7 were waited for; matrix products, arithmetic and copies ran while one was open for 2% of the time, Pallas kernels for 10%

profile of v2, /device:TPU:0, one launch (start us, length us, event | category | flops | bytes accessed | tf_op | source)
XLA Modules:
  0.0 59.4 jit_solution(8531152790498326720)
XLA Ops:
  0.7 4.2 %prep.1 = bf16[4,2,176,256]{3,2,1,0:T(8,128)(2,1)} custom-call(s32[1,1]{1,0:T(1,128)S(6)} %copy.8.rank_ref, bf16[1024,256]{1,0:T(8,128)(2,1)} %bitcast.35, bf16[1,1024,1024]{2,1,0:T(8,128)(2,1)} %bitcast.29, bf16[1024,384]{1,0:T(8,128)(2,1)} %bitcast.33, bf16[1024,256]{1,0:T(8,128)(2,1)} %bitcast.36), custom_call_target="tpu_custom_call" | custom-call | flops 872415232 | bytes 3932160 | tf_op jit(solution)/shard_map/prep/pallas_call | solution.py:192
  4.9 5.2 %all-to-all-start = ((bf16[8,176,256]{2,1,0:T(8,128)(2,1)}), bf16[8,176,256]{2,1,0:T(8,128)(2,1)S(1)}, u32[]{:S(2)}, u32[]{:S(2)}) async-start(bf16[8,176,256]{2,1,0:T(8,128)(2,1)} %bitcast.28), calls=%async_computation | async-start | bytes 1441792 | tf_op jit(solution)/shard_map/all_to_all | solution.py:216
  10.1 0.1 select_reduce_fusion.order_ref
  10.2 0.7 %fusion = (s32[1]{0:T(128)}, s32[1]{0:T(128)}, s32[1]{0:T(128)}) fusion(s32[4]{0:T(128)S(1)} %select_reduce_fusion.order_ref), kind=kLoop, calls=%fused_computation.10 | loop fusion | bytes 24 | tf_op jit(solution)/shard_map/slice | solution.py:253
  13.4 0.1 reshape.17.coup_ref
  14.7 1.1 %weights.1 = (f32[96,256]{1,0:T(8,128)S(1)}, f32[16,256]{1,0:T(8,128)S(1)}) custom-call(s32[4]{0:T(128)S(1)} %select_reduce_fusion.order_ref, s32[4,8,32]{2,1,0:T(8,128)S(1)} %reshape.17.coup_ref), custom_call_target="tpu_custom_call" | custom-call | flops 1048576 | bytes 98304 | tf_op jit(solution)/shard_map/weights/pallas_call | solution.py:221
  15.8 5.2 %full.1 = (f32[1024,384]{1,0:T(8,128)}, bf16[1024,256]{1,0:T(8,128)(2,1)}) custom-call(bf16[1,1024,1024]{2,1,0:T(8,128)(2,1)} %bitcast.30, bf16[1024,384]{1,0:T(8,128)(2,1)} %bitcast.34, bf16[1024,256]{1,0:T(8,128)(2,1)} %bitcast.37), custom_call_target="tpu_custom_call" | custom-call | flops 1342177280 | bytes 5505024 | tf_op jit(solution)/shard_map/full/pallas_call | solution.py:232
  21.0 0.3 all-to-all-done
  21.4 0.7 %pad_maximum_fusion = bf16[2,2,128,256]{3,2,1,0:T(8,128)(2,1)} fusion(bf16[1,2,128,256]{3,2,1,0:T(8,128)(2,1)S(1)} %get-tuple-element.34, bf16[1,2,128,256]{3,2,1,0:T(8,128)(2,1)S(1)} %get-tuple-element.35), kind=kLoop, calls=%fused_computation | loop fusion | flops 131072 | bytes 524288 | tf_op jit(solution)/shard_map/concatenate | solution.py:256
  22.1 0.2 collective-permute-start.3
  24.2 3.7 %collective-permute-start.2 = (bf16[2,48,256]{2,1,0:T(8,128)(2,1)S(1)}, bf16[2,48,256]{2,1,0:T(8,128)(2,1)S(1)}, u32[]{:S(2)}, u32[]{:S(2)}) collective-permute-start(bf16[2,48,256]{2,1,0:T(8,128)(2,1)S(1)} %get-tuple-element.33.refs_0_), channel_id=1, source_target_pairs={{0,6},{2,4},{4,2},{6,0},{1,7},{3,5},{5,3},{7,1},{8,14},{10,12},{12... | collective-permute-start | bytes 147464 | tf_op jit(solution)/shard_map/ppermute | solution.py:261
  27.8 0.8 %collective-permute-start = (bf16[2,48,256]{2,1,0:T(8,128)(2,1)S(1)}, bf16[2,48,256]{2,1,0:T(8,128)(2,1)S(1)}, u32[]{:S(2)}, u32[]{:S(2)}) collective-permute-start(bf16[2,48,256]{2,1,0:T(8,128)(2,1)S(1)} %get-tuple-element.33.refs_0_), channel_id=1, source_target_pairs={{0,2},{2,0},{4,6},{6,4},{1,3},{3,1},{5,7},{7,5},{8,10},{10,8},{12,... | collective-permute-start | bytes 147464 | tf_op jit(solution)/shard_map/ppermute | solution.py:261
  28.6 1.5 %collective-permute-done.2.refs_3_ = bf16[2,48,256]{2,1,0:T(8,128)(2,1)S(1)} collective-permute-done((bf16[2,48,256]{2,1,0:T(8,128)(2,1)S(1)}, bf16[2,48,256]{2,1,0:T(8,128)(2,1)S(1)}, u32[]{:S(2)}, u32[]{:S(2)}) %collective-permute-start.2) | collective-permute-done | bytes 49184 | tf_op jit(solution)/shard_map/ppermute | solution.py:261
  30.2 2.8 %collective-permute-done.1.refs_2_ = bf16[2,48,256]{2,1,0:T(8,128)(2,1)S(1)} collective-permute-done((bf16[2,48,256]{2,1,0:T(8,128)(2,1)S(1)}, bf16[2,48,256]{2,1,0:T(8,128)(2,1)S(1)}, u32[]{:S(2)}, u32[]{:S(2)}) %collective-permute-start.1) | collective-permute-done | bytes 49184 | tf_op jit(solution)/shard_map/ppermute | solution.py:261
  33.0 0.0 collective-permute-done.refs_1_
  33.0 0.2 section_1.1
  33.2 2.2 %collective-permute-start.6 = (bf16[2,48,256]{2,1,0:T(8,128)(2,1)S(1)}, bf16[2,48,256]{2,1,0:T(8,128)(2,1)S(1)}, u32[]{:S(2)}, u32[]{:S(2)}) collective-permute-start(bf16[2,48,256]{2,1,0:T(8,128)(2,1)S(1)} %get-tuple-element.24.refs_4_), channel_id=1, source_target_pairs={{0,6},{2,4},{4,2},{6,0},{1,7},{3,5},{5,3},{7,1},{8,14},{10,12},{12... | collective-permute-start | bytes 147464 | tf_op jit(solution)/shard_map/ppermute | solution.py:261
  35.4 0.3 collective-permute-start.5
  35.7 1.9 %collective-permute-start.4 = (bf16[2,48,256]{2,1,0:T(8,128)(2,1)S(1)}, bf16[2,48,256]{2,1,0:T(8,128)(2,1)S(1)}, u32[]{:S(2)}, u32[]{:S(2)}) collective-permute-start(bf16[2,48,256]{2,1,0:T(8,128)(2,1)S(1)} %get-tuple-element.24.refs_4_), channel_id=1, source_target_pairs={{0,2},{2,0},{4,6},{6,4},{1,3},{3,1},{5,7},{7,5},{8,10},{10,8},{12,... | collective-permute-start | bytes 147464 | tf_op jit(solution)/shard_map/ppermute | solution.py:261
  37.6 1.5 %collective-permute-done.6.refs_7_ = bf16[2,48,256]{2,1,0:T(8,128)(2,1)S(1)} collective-permute-done((bf16[2,48,256]{2,1,0:T(8,128)(2,1)S(1)}, bf16[2,48,256]{2,1,0:T(8,128)(2,1)S(1)}, u32[]{:S(2)}, u32[]{:S(2)}) %collective-permute-start.6) | collective-permute-done | bytes 49184 | tf_op jit(solution)/shard_map/ppermute | solution.py:261
  39.2 1.7 %collective-permute-done.5.refs_6_ = bf16[2,48,256]{2,1,0:T(8,128)(2,1)S(1)} collective-permute-done((bf16[2,48,256]{2,1,0:T(8,128)(2,1)S(1)}, bf16[2,48,256]{2,1,0:T(8,128)(2,1)S(1)}, u32[]{:S(2)}, u32[]{:S(2)}) %collective-permute-start.5) | collective-permute-done | bytes 49184 | tf_op jit(solution)/shard_map/ppermute | solution.py:261
  40.9 0.0 collective-permute-done.4.refs_5_
  40.9 0.3 section_2.1
  41.2 2.3 %collective-permute-start.9 = (bf16[2,48,256]{2,1,0:T(8,128)(2,1)S(1)}, bf16[2,48,256]{2,1,0:T(8,128)(2,1)S(1)}, u32[]{:S(2)}, u32[]{:S(2)}) collective-permute-start(bf16[2,48,256]{2,1,0:T(8,128)(2,1)S(1)} %get-tuple-element.25.refs_8_), channel_id=1, source_target_pairs={{0,6},{2,4},{4,2},{6,0},{1,7},{3,5},{5,3},{7,1},{8,14},{10,12},{12... | collective-permute-start | bytes 147464 | tf_op jit(solution)/shard_map/ppermute | solution.py:261
  43.5 0.1 collective-permute-start.8
  43.5 2.1 %collective-permute-start.7 = (bf16[2,48,256]{2,1,0:T(8,128)(2,1)S(1)}, bf16[2,48,256]{2,1,0:T(8,128)(2,1)S(1)}, u32[]{:S(2)}, u32[]{:S(2)}) collective-permute-start(bf16[2,48,256]{2,1,0:T(8,128)(2,1)S(1)} %get-tuple-element.25.refs_8_), channel_id=1, source_target_pairs={{0,2},{2,0},{4,6},{6,4},{1,3},{3,1},{5,7},{7,5},{8,10},{10,8},{12,... | collective-permute-start | bytes 147464 | tf_op jit(solution)/shard_map/ppermute | solution.py:261
  45.6 1.5 %collective-permute-done.9.refs_11_ = bf16[2,48,256]{2,1,0:T(8,128)(2,1)S(1)} collective-permute-done((bf16[2,48,256]{2,1,0:T(8,128)(2,1)S(1)}, bf16[2,48,256]{2,1,0:T(8,128)(2,1)S(1)}, u32[]{:S(2)}, u32[]{:S(2)}) %collective-permute-start.9) | collective-permute-done | bytes 49184 | tf_op jit(solution)/shard_map/ppermute | solution.py:261
  47.1 1.6 %collective-permute-done.8.refs_10_ = bf16[2,48,256]{2,1,0:T(8,128)(2,1)S(1)} collective-permute-done((bf16[2,48,256]{2,1,0:T(8,128)(2,1)S(1)}, bf16[2,48,256]{2,1,0:T(8,128)(2,1)S(1)}, u32[]{:S(2)}, u32[]{:S(2)}) %collective-permute-start.8) | collective-permute-done | bytes 49184 | tf_op jit(solution)/shard_map/ppermute | solution.py:261
  48.7 0.0 collective-permute-done.7.refs_9_
  48.7 0.3 last_sums.1
  49.0 9.2 %all_to_all.20 = bf16[8,48,256]{2,1,0:T(8,128)(2,1)S(1)} all-to-all(bf16[8,48,256]{2,1,0:T(8,128)(2,1)S(1)} %bitcast.27), channel_id=1, replica_groups=mesh['level'=4,'z'=4,'x'=2] {'level','x'}, dimensions={0} | all-to-all | bytes 393216 | tf_op jit(solution)/shard_map/all_to_all | solution.py:293
  58.3 1.2 %final.1 = bf16[1024,384]{1,0:T(8,128)(2,1)} custom-call(bf16[384,256]{1,0:T(8,128)(2,1)S(1)} %bitcast.26, f32[1024,384]{1,0:T(8,128)S(1)} %copy-done, bf16[1024,256]{1,0:T(8,128)(2,1)S(1)} %copy-done.1), custom_call_target="tpu_custom_call" | custom-call | flops 201326592 | bytes 2883584 | tf_op jit(solution)/shard_map/final/pallas_call | solution.py:298
  (13 shorter events, 0.1 us)
Async XLA Ops:
  0.7 9.4 %copy-start.3 = (s32[4]{0:T(128)S(1)}, s32[4]{0:T(128)}, u32[]{:S(2)}) copy-start(s32[4]{0:T(128)} %param.13) | copy-start | bytes 52
  0.7 12.7 %copy-start.2 = (s32[4,8,4,8]{3,2,1,0:T(4,128)S(1)}, s32[4,8,4,8]{3,2,1,0:T(4,128)}, u32[]{:S(2)}) copy-start(s32[4,8,4,8]{3,2,1,0:T(4,128)} %param.12) | copy-start | bytes 12292
  4.9 16.5 %all-to-all-start = ((bf16[8,176,256]{2,1,0:T(8,128)(2,1)}), bf16[8,176,256]{2,1,0:T(8,128)(2,1)S(1)}, u32[]{:S(2)}, u32[]{:S(2)}) async-start(bf16[8,176,256]{2,1,0:T(8,128)(2,1)} %bitcast.28), calls=%async_computation | async-start | bytes 1441792 | tf_op jit(solution)/shard_map/all_to_all | solution.py:216
  21.3 36.9 %copy-start = (f32[1024,384]{1,0:T(8,128)S(1)}, f32[1024,384]{1,0:T(8,128)}, u32[]{:S(2)}) copy-start(f32[1024,384]{1,0:T(8,128)} %get-tuple-element.29.dr_ref) | copy-start | bytes 4718596
  21.4 36.9 %copy-start.1 = (bf16[1024,256]{1,0:T(8,128)(2,1)S(1)}, bf16[1024,256]{1,0:T(8,128)(2,1)}, u32[]{:S(2)}) copy-start(bf16[1024,256]{1,0:T(8,128)(2,1)} %get-tuple-element.30.de_ref) | copy-start | bytes 1572868
  22.1 6.5 %collective-permute-start.3 = (bf16[2,2,128,256]{3,2,1,0:T(8,128)(2,1)}, bf16[2,2,128,256]{3,2,1,0:T(8,128)(2,1)S(1)}, u32[]{:S(2)}, u32[]{:S(2)}) collective-permute-start(bf16[2,2,128,256]{3,2,1,0:T(8,128)(2,1)} %pad_maximum_fusion), channel_id=1, source_target_pairs={{0,8},{8,0},{16,24},{24,16},{1,9},{9,1},{17,25},{25,17},{2,10},{10... | collective-permute-start | bytes 786440 | tf_op jit(solution)/shard_map/ppermute | solution.py:257
  24.2 6.0 %collective-permute-start.2 = (bf16[2,48,256]{2,1,0:T(8,128)(2,1)S(1)}, bf16[2,48,256]{2,1,0:T(8,128)(2,1)S(1)}, u32[]{:S(2)}, u32[]{:S(2)}) collective-permute-start(bf16[2,48,256]{2,1,0:T(8,128)(2,1)S(1)} %get-tuple-element.33.refs_0_), channel_id=1, source_target_pairs={{0,6},{2,4},{4,2},{6,0},{1,7},{3,5},{5,3},{7,1},{8,14},{10,12},{12... | collective-permute-start | bytes 147464 | tf_op jit(solution)/shard_map/ppermute | solution.py:261
  27.8 5.1 %collective-permute-start.1 = (bf16[2,48,256]{2,1,0:T(8,128)(2,1)S(1)}, bf16[2,48,256]{2,1,0:T(8,128)(2,1)S(1)}, u32[]{:S(2)}, u32[]{:S(2)}) collective-permute-start(bf16[2,48,256]{2,1,0:T(8,128)(2,1)S(1)} %get-tuple-element.33.refs_0_), channel_id=1, source_target_pairs={{0,4},{2,6},{4,0},{6,2},{1,5},{3,7},{5,1},{7,3},{8,12},{10,14},{12... | collective-permute-start | bytes 147464 | tf_op jit(solution)/shard_map/ppermute | solution.py:261
  27.8 5.1 %collective-permute-start = (bf16[2,48,256]{2,1,0:T(8,128)(2,1)S(1)}, bf16[2,48,256]{2,1,0:T(8,128)(2,1)S(1)}, u32[]{:S(2)}, u32[]{:S(2)}) collective-permute-start(bf16[2,48,256]{2,1,0:T(8,128)(2,1)S(1)} %get-tuple-element.33.refs_0_), channel_id=1, source_target_pairs={{0,2},{2,0},{4,6},{6,4},{1,3},{3,1},{5,7},{7,5},{8,10},{10,8},{12,... | collective-permute-start | bytes 147464 | tf_op jit(solution)/shard_map/ppermute | solution.py:261
  33.2 6.0 %collective-permute-start.6 = (bf16[2,48,256]{2,1,0:T(8,128)(2,1)S(1)}, bf16[2,48,256]{2,1,0:T(8,128)(2,1)S(1)}, u32[]{:S(2)}, u32[]{:S(2)}) collective-permute-start(bf16[2,48,256]{2,1,0:T(8,128)(2,1)S(1)} %get-tuple-element.24.refs_4_), channel_id=1, source_target_pairs={{0,6},{2,4},{4,2},{6,0},{1,7},{3,5},{5,3},{7,1},{8,14},{10,12},{12... | collective-permute-start | bytes 147464 | tf_op jit(solution)/shard_map/ppermute | solution.py:261
  35.4 5.4 %collective-permute-start.5 = (bf16[2,48,256]{2,1,0:T(8,128)(2,1)S(1)}, bf16[2,48,256]{2,1,0:T(8,128)(2,1)S(1)}, u32[]{:S(2)}, u32[]{:S(2)}) collective-permute-start(bf16[2,48,256]{2,1,0:T(8,128)(2,1)S(1)} %get-tuple-element.24.refs_4_), channel_id=1, source_target_pairs={{0,4},{2,6},{4,0},{6,2},{1,5},{3,7},{5,1},{7,3},{8,12},{10,14},{12... | collective-permute-start | bytes 147464 | tf_op jit(solution)/shard_map/ppermute | solution.py:261
  35.7 5.2 %collective-permute-start.4 = (bf16[2,48,256]{2,1,0:T(8,128)(2,1)S(1)}, bf16[2,48,256]{2,1,0:T(8,128)(2,1)S(1)}, u32[]{:S(2)}, u32[]{:S(2)}) collective-permute-start(bf16[2,48,256]{2,1,0:T(8,128)(2,1)S(1)} %get-tuple-element.24.refs_4_), channel_id=1, source_target_pairs={{0,2},{2,0},{4,6},{6,4},{1,3},{3,1},{5,7},{7,5},{8,10},{10,8},{12,... | collective-permute-start | bytes 147464 | tf_op jit(solution)/shard_map/ppermute | solution.py:261
  41.2 5.9 %collective-permute-start.9 = (bf16[2,48,256]{2,1,0:T(8,128)(2,1)S(1)}, bf16[2,48,256]{2,1,0:T(8,128)(2,1)S(1)}, u32[]{:S(2)}, u32[]{:S(2)}) collective-permute-start(bf16[2,48,256]{2,1,0:T(8,128)(2,1)S(1)} %get-tuple-element.25.refs_8_), channel_id=1, source_target_pairs={{0,6},{2,4},{4,2},{6,0},{1,7},{3,5},{5,3},{7,1},{8,14},{10,12},{12... | collective-permute-start | bytes 147464 | tf_op jit(solution)/shard_map/ppermute | solution.py:261
  43.5 5.2 %collective-permute-start.8 = (bf16[2,48,256]{2,1,0:T(8,128)(2,1)S(1)}, bf16[2,48,256]{2,1,0:T(8,128)(2,1)S(1)}, u32[]{:S(2)}, u32[]{:S(2)}) collective-permute-start(bf16[2,48,256]{2,1,0:T(8,128)(2,1)S(1)} %get-tuple-element.25.refs_8_), channel_id=1, source_target_pairs={{0,4},{2,6},{4,0},{6,2},{1,5},{3,7},{5,1},{7,3},{8,12},{10,14},{12... | collective-permute-start | bytes 147464 | tf_op jit(solution)/shard_map/ppermute | solution.py:261
  43.5 5.2 %collective-permute-start.7 = (bf16[2,48,256]{2,1,0:T(8,128)(2,1)S(1)}, bf16[2,48,256]{2,1,0:T(8,128)(2,1)S(1)}, u32[]{:S(2)}, u32[]{:S(2)}) collective-permute-start(bf16[2,48,256]{2,1,0:T(8,128)(2,1)S(1)} %get-tuple-element.25.refs_8_), channel_id=1, source_target_pairs={{0,2},{2,0},{4,6},{6,4},{1,3},{3,1},{5,7},{7,5},{8,10},{10,8},{12,... | collective-permute-start | bytes 147464 | tf_op jit(solution)/shard_map/ppermute | solution.py:261
